TPU v7x, 32 devices: a whole 2x2x4 slice. The times are simulated.
32 devices in a mesh: gx: 2 (over x), gy: 4 (over y, core), gz: 4 (over z).
Axes of the slice: x: 2, y: 2, z: 4, core: 2. Of those that a mesh axis runs over, the one named last changes fastest.
Arguments:
- images: bfloat16 [32, 5, 524288], P(('gx', 'gy', 'gz')), may hold values from 0 to 0.125
- order: int32 [32], replicated, may hold values from 0 to 31, as said below
Outputs:
- frame: float32 [5, 524288], P(None, 'gx')
Inputs may be any that keep to these rules, and one draw needn't show every extreme that they name: order is a permutation of the bricks, where brick r sits at index r // 16 along gx, (r // 4) % 4 along gy and r % 4 along gz; the bricks of one gz index take consecutive places, within them the bricks of one (gy, gz) pair take consecutive places; the order of gz indices, the order of gy indices within each gz index and the order of gx indices within each (gy, gz) pair are arbitrary and may differ from slab to slab and from column to column.
All inputs are finite; a program needn't handle non-finite values.
Results may differ from a plain program's by a relative error of at most 0.0003.
Values may be sent and summed in bfloat16 or wider, within the bound.
A program may use at most 64 MiB of HBM per device.

v0:
```python
import jax
import jax.numpy as jnp
from jax import lax
from jax.sharding import PartitionSpec as P


def composite(stacked, member_keys):
    ranked = jnp.argsort(member_keys)

    def layer(total, member):
        picture = lax.dynamic_index_in_dim(stacked, member, 0, keepdims=False).astype(jnp.float32)
        return (total + (1.0 - total[4:5]) * picture, None)

    start = jnp.zeros(stacked.shape[1:], jnp.float32)
    total, _ = lax.scan(layer, start, ranked)
    return total[None]


def per_device(images, order):
    count_x = lax.axis_size("gx")
    count_y = lax.axis_size("gy")
    count_z = lax.axis_size("gz")
    bricks_all = count_x * count_y * count_z
    place_z = lax.axis_index("gz")
    grid_order = order.reshape(count_x, count_y, count_z)
    column_order = lax.dynamic_index_in_dim(grid_order, place_z, 2, keepdims=False)
    pixels = images.shape[2]
    layers = images.reshape(1, images.shape[1], bricks_all, pixels // bricks_all)
    joined_keys = column_order.reshape(-1)
    partial_value = composite(
        lax.all_to_all(layers, ("gx", "gy"), split_axis=2, concat_axis=0, tiled=True), joined_keys
    )
    slab_keys = jnp.min(grid_order, axis=(0, 1))
    partial_value = composite(
        lax.all_to_all(partial_value, "gz", split_axis=2, concat_axis=0, tiled=True), slab_keys
    )
    tiles = lax.all_gather(partial_value, ("gy", "gz"), axis=2, tiled=True)
    return tiles.reshape(tiles.shape[1], -1)


def solution(mesh):
    in_specs = (P(("gx", "gy", "gz"), None, None), P())
    out_specs = P(None, "gx")
    return jax.shard_map(
        per_device, mesh=mesh, in_specs=in_specs, out_specs=out_specs, check_vma=False
    )
```

profile of v0, /device:TPU:0, one launch (start us, length us, event | category | flops | bytes accessed | tf_op | source)
XLA Modules:
  0.0 295.9 jit_solution(15883542343164375677)
XLA Ops:
  6.5 5.3 %all-to-all-start = ((bf16[1,5,32,16384]{3,1,0,2:T(8,128)(2,1)}), bf16[1,5,32,16384]{3,1,0,2:T(8,128)(2,1)}, u32[]{:S(2)}, u32[]{:S(2)}) async-start(bf16[1,5,32,16384]{3,1,0,2:T(8,128)(2,1)} %bitcast.44), calls=%async_computation | async-start | bytes 16777216 | tf_op jit(solution)/shard_map/all_to_all | solution.py:31
  12.3 1.0 sort.35
  13.2 92.2 %all-to-all-done = bf16[1,5,32,16384]{3,1,0,2:T(8,128)(2,1)} async-done(((bf16[1,5,32,16384]{3,1,0,2:T(8,128)(2,1)}), bf16[1,5,32,16384]{3,1,0,2:T(8,128)(2,1)}, u32[]{:S(2)}, u32[]{:S(2)}) %all-to-all-start) | async-done | bytes 5242912 | tf_op jit(solution)/shard_map/all_to_all | solution.py:31
  105.4 10.4 %copy.29 = bf16[1,5,8,4,16384]{4,3,1,2,0:T(4,128)(2,1)} copy(bf16[1,5,8,4,16384]{4,1,3,2,0:T(8,128)(2,1)} %bitcast.1) | data formatting | bytes 10485760 | tf_op jit(solution)/shard_map/all_to_all | solution.py:31
  115.8 39.8 %while.22 = (s32[]{:T(128)}, f32[5,4,16384]{2,1,0:T(4,128)S(1)}, s32[8]{0:T(128)S(1)}, bf16[8,5,4,16384]{3,2,1,0:T(4,128)(2,1)}, s32[]{:T(128)}, /*index=5*/s32[]{:T(128)}, s32[]{:T(128)}) while((s32[]{:T(128)}, f32[5,4,16384]{2,1,0:T(4,128)S(1)}, s32[8]{0:T(128)S(1)}, bf16[8,5,4,16384]{3,2,1,0:T(4,128)(2,1)}, s32[]{:T(128)}, ...), condition=%wide.region_4.5_spmd.clone, body=%wide.region_3.4_spmd.clone.sunk | while | flops 1703942 | bytes 6684818 | solution.py:15
  115.8 0.7 dynamic_slice.33
  118.9 1.8 fusion.7
  120.8 0.7 dynamic_slice.33
  123.9 1.8 fusion.7
  125.8 0.7 dynamic_slice.33
  128.9 1.8 fusion.7
  130.7 0.7 dynamic_slice.33
  133.9 1.8 fusion.7
  135.7 0.7 dynamic_slice.33
  138.8 1.8 fusion.7
  140.7 0.7 dynamic_slice.33
  143.8 1.8 fusion.7
  145.7 0.7 dynamic_slice.33
  148.8 1.8 fusion.7
  150.6 0.7 dynamic_slice.33
  153.8 1.8 fusion.7
  155.6 2.4 copy.20
  158.0 5.7 %all-to-all-start.1 = ((f32[1,5,4,16384]{3,0,1,2:T(1,128)}), f32[1,5,4,16384]{3,0,1,2:T(1,128)S(1)}, u32[]{:S(2)}, u32[]{:S(2)}) async-start(f32[1,5,4,16384]{3,0,1,2:T(1,128)} %copy.20), calls=%async_computation.1 | async-start | bytes 2621440 | tf_op jit(solution)/shard_map/all_to_all | solution.py:35
  163.7 0.7 sort.34
  164.5 30.3 %all-to-all-done.1 = f32[1,5,4,16384]{3,0,1,2:T(1,128)S(1)} async-done(((f32[1,5,4,16384]{3,0,1,2:T(1,128)}), f32[1,5,4,16384]{3,0,1,2:T(1,128)S(1)}, u32[]{:S(2)}, u32[]{:S(2)}) %all-to-all-start.1) | async-done | bytes 1310752 | tf_op jit(solution)/shard_map/all_to_all | solution.py:35
  194.7 0.8 copy.30
  195.6 14.0 %while.23 = (s32[]{:T(128)}, f32[5,1,16384]{2,1,0:T(1,128)S(1)}, s32[4]{0:T(128)S(1)}, f32[4,5,1,16384]{3,0,1,2:T(4,128)S(1)}, s32[]{:T(128)}, /*index=5*/s32[]{:T(128)}, s32[]{:T(128)}) while((s32[]{:T(128)}, f32[5,1,16384]{2,1,0:T(1,128)S(1)}, s32[4]{0:T(128)S(1)}, f32[4,5,1,16384]{3,0,1,2:T(4,128)S(1)}, s32[]{:T(128)}, ...), condition=%wide.region_6.7_spmd.clone, body=%wide.region_5.6_spmd.clone.sunk | while | flops 344070 | bytes 1835154 | solution.py:15
  195.6 0.6 dynamic_slice.35
  206.1 0.6 dynamic_slice.35
  209.6 1.0 copy.23
  210.7 72.6 %all-gather.3.cloned.1.call-done = f32[5,16,16384]{2,0,1:T(8,128)} async-done(((f32[5,1,16384]{2,0,1:T(8,128)}), f32[5,16,16384]{2,0,1:T(8,128)}) %all-gather.3.cloned.1.call-update) | async-done | bytes 5242896 | tf_op jit(solution)/shard_map/all_gather | solution.py:37
  283.2 5.9 %copy.44 = f32[5,262144]{1,0:T(8,128)} copy(f32[5,262144]{1,0:T(8,128)} %bitcast.45) | data formatting | bytes 10485760
  (42 shorter events, 8.3 us)
Async XLA Ops:
  6.5 5.3 %copy-start = (s32[32]{0:T(128)S(1)}, s32[32]{0:T(128)}, u32[]{:S(2)}) copy-start(s32[32]{0:T(128)} %param.7) | copy-start | bytes 388
  6.5 98.9 %all-to-all-start = ((bf16[1,5,32,16384]{3,1,0,2:T(8,128)(2,1)}), bf16[1,5,32,16384]{3,1,0,2:T(8,128)(2,1)}, u32[]{:S(2)}, u32[]{:S(2)}) async-start(bf16[1,5,32,16384]{3,1,0,2:T(8,128)(2,1)} %bitcast.44), calls=%async_computation | async-start | bytes 16777216 | tf_op jit(solution)/shard_map/all_to_all | solution.py:31
  158.0 36.7 %all-to-all-start.1 = ((f32[1,5,4,16384]{3,0,1,2:T(1,128)}), f32[1,5,4,16384]{3,0,1,2:T(1,128)S(1)}, u32[]{:S(2)}, u32[]{:S(2)}) async-start(f32[1,5,4,16384]{3,0,1,2:T(1,128)} %copy.20), calls=%async_computation.1 | async-start | bytes 2621440 | tf_op jit(solution)/shard_map/all_to_all | solution.py:35
  163.7 119.6 %all-gather.3.cloned.1.call-start = ((), (), s32[]{:S(2)}) async-start(), calls=%async_computation.2 | async-start | bytes 8912896 | tf_op jit(solution)/shard_map/all_gather | solution.py:37
Sparse Core Ops, SparseCore 0:
  210.8 72.4 all-gather.2
where the time goes:
time: 297 us; the launch traced here: 296 us
  waiting for transfers between devices  195 us (66%)
  local copies, waits for them, and re-layouts  28.6 us (10%)
  loops' own time  24.8 us (8%)
  other arithmetic  23.1 us (8%)
  between operations  13.4 us (5%)
  starting transfers between devices  11 us (4%)
    all_to_all x1, waiting for transfers between devices, per_device(): lax.all_to_all(layers, ('gx', 'gy'), split_axis=2, concat_axis=0, tiled=T...  92.2 us
    all_gather x1, waiting for transfers between devices, per_device(): tiles = lax.all_gather(partial_value, ('gy', 'gz'), axis=2, tiled=True)  72.6 us
    all_to_all x1, waiting for transfers between devices, per_device(): lax.all_to_all(partial_value, 'gz', split_axis=2, concat_axis=0, tiled=True)  30.3 us
    another operation x2, loops' own time, composite(): total, _ = lax.scan(layer, start, ranked)  24.8 us
    add x12, other arithmetic, layer(): return (total + (1.0 - total[4:5]) * picture, None)  17 us
    all_to_all x1, local copies, waits for them, and re-layouts, per_device(): lax.all_to_all(layers, ('gx', 'gy'), split_axis=2, concat_axis=0, tiled=T...  10.4 us
    dynamic_slice x12, local copies, waits for them, and re-layouts, composite(): total, _ = lax.scan(layer, start, ranked)  7.7 us
  transfers between devices with their start and end apart: 3, of which 3 were waited for; matrix products, arithmetic and copies ran while one was open for 1% of the time, Pallas kernels for 0%

commit v1 on v0

v1 whole, which is shorter than its diff:
```python
import functools

import jax
import jax.numpy as jnp
from jax import lax
from jax.experimental import pallas as pl
from jax.experimental.pallas import tpu as pltpu
from jax.sharding import PartitionSpec as P

MESH = pl.DeviceIdType.MESH
AXES = ("gx", "gy", "gz")
CHUNKS = 8


def span(start, size):
    return pl.ds(pl.multiple_of(start, 128), size)


def front_flags(keys):
    return [[None if i == j else jnp.where(a < b, 1.0, 0.0) for j, b in enumerate(keys)] for i, a in enumerate(keys)]


def blend(pictures, flags):
    alphas = [p[4:5] for p in pictures]
    total = None
    for j, picture in enumerate(pictures):
        clear = None
        for i, alpha in enumerate(alphas):
            if i != j:
                factor = 1.0 - flags[i][j] * alpha
                clear = factor if clear is None else clear * factor
        term = picture if clear is None else clear * picture
        total = term if total is None else total + term
    return total


def kernel(counts, chunks, order_ref, images_ref, out_ref, own, near, pair, side, slab, deep, done,
           load_sem, s1, r1, s2, r2, s3, r3, s4, r4, s5, r5, put_sem):
    nx, ny, nz = counts
    x, y, z = (lax.axis_index(a) for a in AXES)
    band = out_ref.shape[1]
    size = band // chunks
    strip = size // ny
    tile = strip // nz

    barrier = pltpu.get_barrier_semaphore()
    greeted = 0
    for name, me, n in zip(AXES, (x, y, z), counts):
        for d in range(1, n):
            pl.semaphore_signal(barrier, inc=1, device_id={name: lax.rem(me + d, n)}, device_id_type=MESH)
            greeted += 1
    loads = [
        pltpu.make_async_copy(
            images_ref.at[0, :, span(x * band + k * size, size)], own.at[:, span(k * size, size)], load_sem.at[k])
        for k in range(chunks)
    ]
    for c in loads:
        c.start()
    pl.semaphore_wait(barrier, greeted)

    def remote(src, dst, send, recv, name, peer):
        return pltpu.make_async_remote_copy(
            src_ref=src, dst_ref=dst, send_sem=send, recv_sem=recv, device_id={name: peer}, device_id_type=MESH)

    def behind(me, d, n):
        return lax.rem(me + n - d, n)

    def place(px, py, pz):
        return order_ref[(px * ny + py) * nz + pz]

    flags_x = front_flags([place(behind(x, d, nx), y, z) for d in range(nx)])
    flags_y = front_flags([place(0, behind(y, d, ny), z) for d in range(ny)])
    flags_z = front_flags([place(0, 0, behind(z, d, nz)) for d in range(nz)])

    first, second, third, fourth, fifth = {}, {}, {}, {}, {}
    for k in range(chunks):
        for d in range(1, nx):
            peer = lax.rem(x + d, nx)
            c = remote(images_ref.at[0, :, span(peer * band + k * size, size)],
                       near.at[d - 1, :, span(k * size, size)], s1.at[k, d - 1], r1.at[k, d - 1], "gx", peer)
            c.start()
            first[k, d] = c

    def sweep(total, body):
        step = min(total, 1024)

        @pl.loop(0, total // step)
        def _(i):
            body(i * step, step)

    def stage_pair(k):
        loads[k].wait()
        for d in range(1, nx):
            first[k, d].wait_recv()

        def body(at, step):
            here = span(k * size + at, step)
            pictures = [own[:, here].astype(jnp.float32)]
            pictures += [near[d - 1, :, here].astype(jnp.float32) for d in range(1, nx)]
            pair[:, here] = blend(pictures, flags_x)

        sweep(size, body)
        for d in range(1, ny):
            peer = lax.rem(y + d, ny)
            c = remote(pair.at[:, span(k * size + peer * strip, strip)],
                       side.at[d - 1, :, span(k * strip, strip)], s2.at[k, d - 1], r2.at[k, d - 1], "gy", peer)
            c.start()
            second[k, d] = c

    def stage_slab(k):
        for d in range(1, ny):
            second[k, d].wait_recv()

        def body(at, step):
            here = span(k * strip + at, step)
            pictures = [pair[:, span(k * size + y * strip + at, step)]]
            pictures += [side[d - 1, :, here] for d in range(1, ny)]
            slab[:, here] = blend(pictures, flags_y)

        sweep(strip, body)
        for d in range(1, nz):
            peer = lax.rem(z + d, nz)
            c = remote(slab.at[:, span(k * strip + peer * tile, tile)],
                       deep.at[d - 1, :, span(k * tile, tile)], s3.at[k, d - 1], r3.at[k, d - 1], "gz", peer)
            c.start()
            third[k, d] = c

    def stage_tile(k):
        for d in range(1, nz):
            third[k, d].wait_recv()

        def body(at, step):
            here = span(k * tile + at, step)
            pictures = [slab[:, span(k * strip + z * tile + at, step)]]
            pictures += [deep[d - 1, :, here] for d in range(1, nz)]
            done[:, here] = blend(pictures, flags_z)

        sweep(tile, body)
        here = done.at[:, span(k * tile, tile)]
        there = out_ref.at[:, span(k * size + y * strip + z * tile, tile)]
        put = pltpu.make_async_copy(here, there, put_sem.at[k])
        put.start()
        fourth[k, 0] = put
        for d in range(1, nz):
            c = remote(here, there, s4.at[k, d - 1], r4.at[k, d - 1], "gz", lax.rem(z + d, nz))
            c.start()
            fourth[k, d] = c

    bits = [1 << b for b in reversed(range((ny - 1).bit_length()))]

    def stage_spread(k, at):
        if at == 0:
            fourth[k, 0].wait()
            for d in range(1, nz):
                fourth[k, d].wait_recv()
            held = [0]
        else:
            held = [0]
            for b in bits[:at]:
                held += [m | b for m in held]
            for m in held:
                if m & bits[at - 1]:
                    fifth[k, m].wait_recv()
        if at == len(bits):
            return
        for m in held:
            where = out_ref.at[:, span(k * size + (y ^ m) * strip, strip)]
            arrives = m | bits[at]
            c = remote(where, where, s5.at[k, arrives - 1], r5.at[k, arrives - 1], "gy", y ^ bits[at])
            c.start()
            fifth[k, arrives] = c

    stages = [stage_pair, stage_slab, stage_tile]
    stages += [functools.partial(stage_spread, at=at) for at in range(len(bits) + 1)]
    for t in range(chunks + len(stages) - 1):
        for lag, stage in enumerate(stages):
            if 0 <= t - lag < chunks:
                stage(t - lag)
    for group in (first, second, third, fourth, fifth):
        for (k, d), c in group.items():
            if d:
                c.wait_send()


def per_device(counts, images, order):
    nx, ny, nz = counts
    channels, pixels = images.shape[1:]
    band = pixels // nx
    chunks = min(CHUNKS, band // (ny * nz * 128))
    f32, dma = jnp.float32, pltpu.SemaphoreType.DMA
    return pl.pallas_call(
        functools.partial(kernel, counts, chunks),
        out_shape=jax.ShapeDtypeStruct((channels, band), f32),
        in_specs=[pl.BlockSpec(memory_space=pltpu.SMEM), pl.BlockSpec(memory_space=pl.ANY)],
        out_specs=pl.BlockSpec(memory_space=pl.ANY),
        scratch_shapes=[
            pltpu.VMEM((channels, band), images.dtype),
            pltpu.VMEM((nx - 1, channels, band), images.dtype),
            pltpu.VMEM((channels, band), f32),
            pltpu.VMEM((ny - 1, channels, band // ny), f32),
            pltpu.VMEM((channels, band // ny), f32),
            pltpu.VMEM((nz - 1, channels, band // (ny * nz)), f32),
            pltpu.VMEM((channels, band // (ny * nz)), f32),
            dma((chunks,)),
            dma((chunks, nx - 1)), dma((chunks, nx - 1)),
            dma((chunks, ny - 1)), dma((chunks, ny - 1)),
            dma((chunks, nz - 1)), dma((chunks, nz - 1)),
            dma((chunks, nz - 1)), dma((chunks, nz - 1)),
            dma((chunks, ny - 1)), dma((chunks, ny - 1)),
            dma((chunks,)),
        ],
        compiler_params=pltpu.CompilerParams(
            collective_id=0, has_side_effects=True, vmem_limit_bytes=60 * 1024 * 1024),
    )(order, images)


def solution(mesh):
    counts = tuple(mesh.shape[a] for a in AXES)
    return jax.shard_map(
        functools.partial(per_device, counts), mesh=mesh,
        in_specs=(P(AXES, None, None), P()), out_specs=P(None, "gx"), check_vma=False)
```

time: 297 us -> 166 us (0.56)
  waiting for transfers between devices: 195 us -> 0 us
  Pallas kernels: 0 us -> 160 us
  loops' own time: 24.8 us -> 0 us
  other arithmetic: 23.1 us -> 0 us
  local copies, waits for them, and re-layouts: 28.6 us -> 5.86 us
  between operations: 13.4 us -> 0.01 us
  starting transfers between devices: 11 us -> 0 us
    pallas_call x0 -> x1, Pallas kernels: none -> 160 us  [per_device(): pl.pallas_call(functools.partial(kernel, counts, chunks), out_shape=jax.S...]
    all_to_all x2 -> x0, waiting for transfers between devices: 122 us -> none  [the longest x1 92.2 us: per_device(): lax.all_to_all(layers, ('gx', 'gy'), split_axis=2, concat_axis=0, tiled=T...]
    all_gather x1 -> x0, waiting for transfers between devices: 72.6 us -> none  [per_device(): tiles = lax.all_gather(partial_value, ('gy', 'gz'), axis=2, tiled=True)]
    another operation x2 -> x0, loops' own time: 24.8 us -> none  [composite(): total, _ = lax.scan(layer, start, ranked)]
    add x12 -> x0, other arithmetic: 17 us -> none  [layer(): return (total + (1.0 - total[4:5]) * picture, None)]
    all_to_all x2 -> x0, local copies, waits for them, and re-layouts: 11.2 us -> none  [the longest x1 10.4 us: per_device(): lax.all_to_all(layers, ('gx', 'gy'), split_axis=2, concat_axis=0, tiled=T...]
    all_to_all x2 -> x0, starting transfers between devices: 11 us -> none  [the longest x1 5.67 us: per_device(): lax.all_to_all(partial_value, 'gz', split_axis=2, concat_axis=0, tiled=True)]
    dynamic_slice x13 -> x0, local copies, waits for them, and re-layouts: 7.92 us -> none  [the longest x12 7.7 us: composite(): total, _ = lax.scan(layer, start, ranked)]
  transfers between devices with their start and end apart: 3 -> 0, of which waited for: 3 -> 0; matrix products, arithmetic and copies ran while one was open for 1% -> 0% of each run, Pallas kernels for 0% -> 0%
where the time goes in v1:
time: 166 us
  Pallas kernels  160 us (96%)
  local copies, waits for them, and re-layouts  5.86 us (4%)
    pallas_call x1, Pallas kernels, per_device(): pl.pallas_call(functools.partial(kernel, counts, chunks), out_shape=jax.S...  160 us
    unnamed x1, local copies, waits for them, and re-layouts  5.86 us

profile of v1, /device:TPU:0, one launch (start us, length us, event | category | flops | bytes accessed | tf_op | source)
XLA Modules:
  0.0 165.6 jit_solution(8826596237328405605)
XLA Ops:
  0.0 159.7 %shard_map.28 = f32[5,262144]{1,0:T(8,128)} custom-call(s32[32]{0:T(128)} %order_ref.1, bf16[1,5,524288]{2,1,0:T(8,128)(2,1)} %images_ref.1), custom_call_target="tpu_custom_call" | custom-call | tf_op jit(solution)/shard_map/pallas_call | solution.py:191
  159.7 5.9 %copy.4 = f32[5,262144]{1,0:T(8,128)} copy(f32[5,262144]{1,0:T(8,128)} %shard_map.28) | data formatting | bytes 10485760

commit v2 on v1

v2 whole, which is shorter than its diff:
```python
import functools

import jax
import jax.numpy as jnp
from jax import lax
from jax.experimental import pallas as pl
from jax.experimental.pallas import tpu as pltpu
from jax.sharding import PartitionSpec as P

MESH = pl.DeviceIdType.MESH
AXES = ("gx", "gy", "gz")
CHUNKS = 8
PLANS = (0,)


LANES = 128
GROUP = 16


def span(start, size, unit):
    return pl.ds(pl.multiple_of(start, unit), size)


def front_flags(keys):
    return [[None if i == j else jnp.where(a < b, 1.0, 0.0) for j, b in enumerate(keys)] for i, a in enumerate(keys)]


def blend(pictures, flags):
    alphas = [p[4] for p in pictures]
    total = None
    for j, picture in enumerate(pictures):
        clear = None
        for i, alpha in enumerate(alphas):
            if i != j:
                factor = 1.0 - flags[i][j] * alpha
                clear = factor if clear is None else clear * factor
        term = picture if clear is None else [clear * c for c in picture]
        total = term if total is None else [t + c for t, c in zip(total, term)]
    return total


def kernel(counts, chunks, order_ref, images_ref, out_ref, raw, sent, near, pair, side, slab, deep, done, turn,
           load_sem, s1, r1, s2, r2, s3, r3, s4, r4, put_sem):
    nx, ny, nz = counts
    x, y, z = (lax.axis_index(a) for a in AXES)
    channels = out_ref.shape[0]
    band = out_ref.shape[1]
    size = band // chunks
    strip = size // ny
    tile = strip // nz
    f32 = jnp.float32

    barrier = pltpu.get_barrier_semaphore()
    greeted = 0
    for name, me, n in zip(AXES, (x, y, z), counts):
        for d in range(1, n):
            pl.semaphore_signal(barrier, inc=1, device_id={name: lax.rem(me + d, n)}, device_id_type=MESH)
            greeted += 1
    loads = {}
    for k in range(chunks):
        for d in [*range(1, nx), 0]:
            whose = lax.rem(x + d, nx)
            loads[k, d] = pltpu.make_async_copy(
                images_ref.at[0, :, span((whose * band + k * size) * LANES, size * LANES, LANES)],
                raw.at[d, :, span(k * size * LANES, size * LANES, LANES)], load_sem.at[k, d])
            loads[k, d].start()
    pl.semaphore_wait(barrier, greeted)

    def remote(src, dst, send, recv, name, peer):
        return pltpu.make_async_remote_copy(
            src_ref=src, dst_ref=dst, send_sem=send, recv_sem=recv, device_id={name: peer}, device_id_type=MESH)

    def behind(me, d, n):
        return lax.rem(me + n - d, n)

    def place(px, py, pz):
        return order_ref[(px * ny + py) * nz + pz]

    flags_x = front_flags([place(behind(x, d, nx), y, z) for d in range(nx)])
    flags_y = front_flags([place(0, behind(y, d, ny), z) for d in range(ny)])
    flags_z = front_flags([place(0, 0, behind(z, d, nz)) for d in range(nz)])
    first, second, third, gathered = {}, {}, {}, {}

    def sweep(total, step, body, unroll=1):
        lax.fori_loop(0, total // step, lambda i, _: (body(i * step), 0)[1], 0, unroll=unroll)

    def spread_rows(k, d):
        def body(at):
            value = raw[d, :, span((k * size + at) * LANES, 8 * LANES, LANES)].astype(f32)
            for t in range(8):
                turn[span((at + t) * 8, channels, 8), :] = value[:, t * LANES:(t + 1) * LANES]
        sweep(size, 8, body, 2)

    def turned(at, rows):
        return [
            jnp.concatenate([turn[pl.ds((at + r) * 8 + c, 8, stride=8), :] for r in range(0, rows, 8)], axis=0)
            for c in range(channels)
        ]

    def stage_send(k):
        for d in range(1, nx):
            loads[k, d].wait()
            spread_rows(k, d)

            def body(at):
                for c, value in enumerate(turned(at, GROUP)):
                    sent[d - 1, c, span(k * size + at, GROUP, GROUP), :] = value.astype(sent.dtype)
            sweep(size, GROUP, body, 2)
            here = span(k * size, size, GROUP)
            first[k, d] = remote(sent.at[d - 1, :, here], near.at[d - 1, :, here],
                                 s1.at[k, d - 1], r1.at[k, d - 1], "gx", lax.rem(x + d, nx))
            first[k, d].start()

    def stage_pair(k):
        loads[k, 0].wait()
        spread_rows(k, 0)
        for d in range(1, nx):
            first[k, d].wait_recv()

        def body(at):
            here = span(k * size + at, GROUP, GROUP)
            pictures = [turned(at, GROUP)]
            pictures += [[near[d - 1, c, here, :].astype(f32) for c in range(channels)] for d in range(1, nx)]
            for c, value in enumerate(blend(pictures, flags_x)):
                pair[c, here, :] = value
        sweep(size, GROUP, body)
        for d in range(1, ny):
            peer = lax.rem(y + d, ny)
            second[k, d] = remote(pair.at[:, span(k * size + peer * strip, strip, 8), :],
                                  side.at[d - 1, :, span(k * strip, strip, 8), :],
                                  s2.at[k, d - 1], r2.at[k, d - 1], "gy", peer)
            second[k, d].start()

    def stage_slab(k):
        for d in range(1, ny):
            second[k, d].wait_recv()

        def body(at):
            here = span(k * strip + at, 8, 8)
            pictures = [[pair[c, span(k * size + y * strip + at, 8, 8), :] for c in range(channels)]]
            pictures += [[side[d - 1, c, here, :] for c in range(channels)] for d in range(1, ny)]
            for c, value in enumerate(blend(pictures, flags_y)):
                slab[c, here, :] = value
        sweep(strip, 8, body)
        for d in range(1, nz):
            peer = lax.rem(z + d, nz)
            third[k, d] = remote(slab.at[:, span(k * strip + peer * tile, tile, 8), :],
                                 deep.at[d - 1, :, span(k * tile, tile, 8), :],
                                 s3.at[k, d - 1], r3.at[k, d - 1], "gz", peer)
            third[k, d].start()

    puts = {}

    def stage_tile(k):
        for d in range(1, nz):
            third[k, d].wait_recv()

        def body(at):
            here = span(k * tile + at, 8, 8)
            pictures = [[slab[c, span(k * strip + z * tile + at, 8, 8), :] for c in range(channels)]]
            pictures += [[deep[d - 1, c, here, :] for c in range(channels)] for d in range(1, nz)]
            for c, value in enumerate(blend(pictures, flags_z)):
                done[c, here, :] = value
        sweep(tile, 8, body)
        puts[k] = pltpu.make_async_copy(
            done.at[:, span(k * tile, tile, 8), :],
            out_ref.at[:, span(k * size + y * strip + z * tile, tile, 8), :], put_sem.at[k])
        puts[k].start()
        gather(k, 0)

    bits = [1 << b for b in reversed(range((ny - 1).bit_length()))]
    plans = [["z", *bits], [*bits[:1], "z", *bits[1:]]]

    def gather(k, at):
        plan = plans[PLANS[k % len(PLANS)]]
        masks, wide = [0], False
        for step in plan[:at]:
            if step == "z":
                wide = True
            else:
                masks += [m | step for m in masks]
        if at:
            for (kk, step, *name), c in list(gathered.items()):
                if kk == k and step == at - 1:
                    c.wait_recv()
        if at == len(plan):
            return
        step = plan[at]

        def slot(m, d):
            return m * nz + d
        for m in masks:
            base = k * size + (y ^ m) * strip
            if step == "z":
                ref = out_ref.at[:, span(base + z * tile, tile, 8), :]
                src = done.at[:, span(k * tile, tile, 8), :] if m == 0 else ref
                for d in range(1, nz):
                    c = remote(src, ref, s4.at[k, slot(m, d)], r4.at[k, slot(m, d)], "gz", lax.rem(z + d, nz))
                    c.start()
                    gathered[k, at, m, d] = c
            else:
                if wide:
                    if k in puts:
                        puts.pop(k).wait()
                    ref = src = out_ref.at[:, span(base, strip, 8), :]
                else:
                    ref = out_ref.at[:, span(base + z * tile, tile, 8), :]
                    src = done.at[:, span(k * tile, tile, 8), :] if m == 0 else ref
                n = slot(m | step, 0)
                c = remote(src, ref, s4.at[k, n], r4.at[k, n], "gy", y ^ step)
                c.start()
                gathered[k, at, m, 0] = c

    steps = len(bits) + 1
    stages = [stage_send, stage_pair, stage_slab, stage_tile]
    stages += [functools.partial(gather, at=at) for at in range(1, steps + 1)]
    lags = list(range(len(stages)))
    for t in range(chunks + lags[-1]):
        for lag, stage in zip(lags, stages):
            if 0 <= t - lag < chunks:
                stage(t - lag)
    for c in puts.values():
        c.wait()
    for group in (first, second, third, gathered):
        for c in group.values():
            c.wait_send()


def per_device(counts, images, order):
    nx, ny, nz = counts
    channels, pixels = images.shape[1:]
    band = pixels // nx // LANES
    chunks = min(CHUNKS, band // (ny * nz * 8))
    f32, dma = jnp.float32, pltpu.SemaphoreType.DMA
    frame = pl.pallas_call(
        functools.partial(kernel, counts, chunks),
        out_shape=jax.ShapeDtypeStruct((channels, band, LANES), f32),
        in_specs=[pl.BlockSpec(memory_space=pltpu.SMEM), pl.BlockSpec(memory_space=pl.ANY)],
        out_specs=pl.BlockSpec(memory_space=pl.ANY),
        scratch_shapes=[
            pltpu.VMEM((nx, channels, band * LANES), images.dtype),
            pltpu.VMEM((nx - 1, channels, band, LANES), images.dtype),
            pltpu.VMEM((nx - 1, channels, band, LANES), images.dtype),
            pltpu.VMEM((channels, band, LANES), f32),
            pltpu.VMEM((ny - 1, channels, band // ny, LANES), f32),
            pltpu.VMEM((channels, band // ny, LANES), f32),
            pltpu.VMEM((nz - 1, channels, band // (ny * nz), LANES), f32),
            pltpu.VMEM((channels, band // (ny * nz), LANES), f32),
            pltpu.VMEM((band // chunks * 8, LANES), f32),
            dma((chunks, nx)),
            dma((chunks, nx - 1)), dma((chunks, nx - 1)),
            dma((chunks, ny - 1)), dma((chunks, ny - 1)),
            dma((chunks, nz - 1)), dma((chunks, nz - 1)),
            dma((chunks, ny * nz)), dma((chunks, ny * nz)),
            dma((chunks,)),
        ],
        compiler_params=pltpu.CompilerParams(
            collective_id=0, has_side_effects=True, vmem_limit_bytes=60 * 1024 * 1024),
    )(order, images)
    return frame.reshape(channels, band * LANES)


def solution(mesh):
    counts = tuple(mesh.shape[a] for a in AXES)
    return jax.shard_map(
        functools.partial(per_device, counts), mesh=mesh,
        in_specs=(P(AXES, None, None), P()), out_specs=P(None, "gx"), check_vma=False)
```

time: 166 us -> 117 us (0.70)
  Pallas kernels: 160 us -> 109 us
  local copies, waits for them, and re-layouts: 5.86 us -> 8.64 us
    pallas_call x1, Pallas kernels: 160 us -> 109 us  [per_device(): pl.pallas_call(functools.partial(kernel, counts, chunks), out_shape=jax.S...]
    unnamed x1, local copies, waits for them, and re-layouts: 5.86 us -> 8.64 us
where the time goes in v2:
time: 117 us
  Pallas kernels  109 us (93%)
  local copies, waits for them, and re-layouts  8.64 us (7%)
    pallas_call x1, Pallas kernels, per_device(): pl.pallas_call(functools.partial(kernel, counts, chunks), out_shape=jax.S...  109 us
    unnamed x1, local copies, waits for them, and re-layouts  8.64 us

profile of v2, /device:TPU:0, one launch (start us, length us, event | category | flops | bytes accessed | tf_op | source)
XLA Modules:
  0.0 117.2 jit_solution(11620651459431075112)
XLA Ops:
  0.0 108.5 %shard_map.28 = f32[5,2048,128]{2,1,0:T(8,128)} custom-call(s32[32]{0:T(128)} %order_ref.1, bf16[1,5,524288]{2,1,0:T(8,128)(2,1)} %images_ref.1), custom_call_target="tpu_custom_call" | custom-call | tf_op jit(solution)/shard_map/pallas_call | solution.py:235
  108.5 8.6 %copy.5 = f32[1,5,2048,128]{3,1,2,0:T(8,128)} copy(f32[1,5,2048,128]{3,2,1,0:T(8,128)} %bitcast.4) | data formatting | bytes 10485760
